TPU v7x, 128 devices: a whole 4x4x4 slice. The times are simulated.
128 devices in a mesh: col: 16 (over y, z), row: 8 (over x, core).
Axes of the slice: x: 4, y: 4, z: 4, core: 2. Of those that a mesh axis runs over, the one named last changes fastest.
Arguments:
- u_factors: bfloat16 [2, 64, 256, 64, 128], P(None, 'row', None, 'col'), may hold values from -0.09375 to 0.09375
- v_factors: bfloat16 [2, 64, 256, 64, 128], P(None, 'row', None, 'col'), may hold values from -0.375 to 0.375
- ranks: int32 [2, 64, 64], P(None, 'row', 'col'), may hold values from 8 to 64
- model_init: float32 [2, 16384, 256], P(None, ('col', 'row')), may hold values from -6 to 6
- observed: float32 [2, 16384, 256], P(None, ('row', 'col')), may hold values from -6 to 6
- step: float32 [2], replicated, may hold values from 0.1 to 0.4
Outputs:
- model: float32 [2, 16384, 256], P(None, ('col', 'row'))
- misfit: float32 [2, 16384, 256], P(None, ('row', 'col'))
Inputs may be any that keep to these rules, and one draw needn't show every extreme that they name: `ranks`: columns of a factor beyond its tile's rank do not count.
All inputs are finite; a program needn't handle non-finite values.
Results may differ from a plain program's by a relative error of at most 0.0085.
Values may be sent and summed in bfloat16 or wider, within the bound.
A program may use at most 128 MiB of HBM per device.

v0:
```python
import jax
import jax.numpy as jnp
from jax import lax
from jax.sharding import PartitionSpec as P

ITERS = 2


def split_product(product, rank_mask, rank_most, right_count):
    real = product[..., :rank_most, :right_count] + product[..., rank_most:, right_count:]
    imaginary = product[..., :rank_most, right_count:] - product[..., rank_most:, :right_count]
    weights = rank_mask[..., None]
    return jnp.concatenate([real * weights, imaginary * weights], -1).astype(jnp.bfloat16)


def expand_complex(coefficient, right_count):
    real = coefficient[..., :right_count]
    imaginary = coefficient[..., right_count:]
    upper = jnp.concatenate([real, imaginary], -1)
    lower = jnp.concatenate([-imaginary, real], -1)
    return jnp.concatenate([upper, lower], -2)


def local(u_factors, v_factors, ranks, model_init, observed, step):
    frequencies = model_init.shape[0]
    rank_most = u_factors.shape[-1] // 2
    right_count = model_init.shape[-1] // 2
    tile_size = u_factors.shape[2]
    rows_here = u_factors.shape[1]
    cols_here = u_factors.shape[3]
    rank_mask = (
        jnp.arange(rank_most, dtype=jnp.int32)[None, None, None, :] < ranks[..., None]
    ).astype(jnp.float32)
    model = model_init
    misfit = model_init
    observed_block = lax.all_gather(observed, "col", axis=1, tiled=True)
    for sweep in range(ITERS):
        gathered = lax.all_gather(model.astype(jnp.bfloat16), "row", axis=1, tiled=True)
        model_tiles = gathered.reshape(frequencies, cols_here, tile_size, 2 * right_count)
        product = jnp.einsum(
            "fiajk,fjal->fijkl", v_factors, model_tiles, preferred_element_type=jnp.float32
        )
        coefficient = expand_complex(
            split_product(product, rank_mask, rank_most, right_count), right_count
        )
        partial_value = jnp.einsum(
            "fiajk,fijkl->fial", u_factors, coefficient, preferred_element_type=jnp.float32
        )
        partial_value = partial_value.reshape(frequencies, rows_here * tile_size, 2 * right_count)
        predicted = lax.psum(partial_value, "col")
        full_misfit = predicted - observed_block
        misfit_half = full_misfit.astype(jnp.bfloat16)
        share = observed.shape[1]
        misfit = lax.dynamic_slice_in_dim(full_misfit, lax.axis_index("col") * share, share, 1)
        misfit_tiles = misfit_half.reshape(frequencies, rows_here, tile_size, 2 * right_count)
        product = jnp.einsum(
            "fiajk,fial->fijkl", u_factors, misfit_tiles, preferred_element_type=jnp.float32
        )
        back = expand_complex(
            split_product(product, rank_mask, rank_most, right_count), right_count
        )
        gradient_part = jnp.einsum(
            "fiajk,fijkl->fjal", v_factors, back, preferred_element_type=jnp.float32
        )
        gradient_part = gradient_part.reshape(frequencies, cols_here * tile_size, 2 * right_count)
        gradient = lax.psum_scatter(gradient_part, "row", scatter_dimension=1, tiled=True)
        model = model - step[:, None, None] * gradient
    return (model, misfit)


def solution(mesh):
    return jax.shard_map(
        local,
        mesh=mesh,
        in_specs=(
            P(None, "row", None, "col", None),
            P(None, "row", None, "col", None),
            P(None, "row", "col"),
            P(None, ("col", "row"), None),
            P(None, ("row", "col"), None),
            P(),
        ),
        out_specs=(P(None, ("col", "row"), None), P(None, ("row", "col"), None)),
        check_vma=False,
    )
```

profile of v0, /device:TPU:1, one launch (start us, length us, event | category | flops | bytes accessed | tf_op | source)
XLA Modules:
  0.0 441.2 jit_solution(17294954381206863518)
XLA Ops:
  7.2 0.0 all-gather.4.cloned.1.call-start
  7.2 1.6 convert_element_type.23
  8.8 0.0 all-gather.4.cloned.1.call-update
  8.9 0.0 all-reduce.3.cloned.1.call-start
  8.9 7.5 %copy.8 = bf16[2,8,256,4,128]{2,4,1,3,0:T(8,128)(2,1)} copy(bf16[2,8,256,4,128]{4,3,2,1,0:T(4,128)(2,1)} %param.7) | data formatting | bytes 8388608 | tf_op args[1]
  16.4 7.4 %copy.11 = bf16[2,8,256,4,128]{2,4,3,1,0:T(8,128)(2,1)} copy(bf16[2,8,256,4,128]{4,3,2,1,0:T(4,128)(2,1)} %param.6) | data formatting | bytes 8388608 | tf_op args[0]
  23.8 0.1 fusion.37
  23.8 13.2 %all-gather.4.cloned.1.call-done = bf16[2,1024,256]{2,1,0:T(8,128)(2,1)} async-done(((bf16[2,128,256]{2,1,0:T(8,128)(2,1)}), bf16[2,1024,256]{2,1,0:T(8,128)(2,1)}) %all-gather.4.cloned.1.call-update) | async-done | bytes 1048592 | tf_op jit(solution)/shard_map/all_gather | solution.py:38
  37.1 3.7 fusion.49
  40.8 0.8 fusion.47
  41.6 0.7 fusion.35
  42.3 1.5 copy-done
  43.8 2.9 fusion.18
  46.7 0.0 all-gather.6.cloned.1.call-start
  46.8 0.7 all-gather.6.cloned.1.call-update
  47.5 0.0 reduce-scatter.3.cloned.1.call-start
  47.5 102.2 %all-reduce.3.cloned.1.call-done = f32[2,2048,256]{2,1,0:T(8,128)} async-done(((f32[2,2048,256]{2,1,0:T(8,128)}), f32[2,2048,256]{2,1,0:T(8,128)}) %all-reduce.3.cloned.1.call-update) | async-done | bytes 4194320 | tf_op jit(solution)/shard_map/psum | solution.py:50
  149.7 53.7 %all-gather.6.cloned.1.call-done = f32[2,2048,256]{2,1,0:T(8,128)} async-done(((f32[2,128,256]{2,1,0:T(8,128)}), f32[2,2048,256]{2,1,0:T(8,128)}) %all-gather.6.cloned.1.call-update) | async-done | bytes 4194320 | tf_op jit(solution)/shard_map/all_gather | solution.py:36
  203.4 4.3 subtract_convert_fusion
  207.7 0.3 copy-done.1
  208.1 1.3 fusion.50
  209.3 1.0 copy.31
  210.3 0.8 fusion.45
  211.1 0.7 fusion.31
  211.8 1.5 copy-done.4
  213.3 2.8 fusion
  216.1 0.0 all-gather.8.cloned.1.call-start
  216.2 30.8 %reduce-scatter.3.cloned.1.call-done = f32[2,128,256]{2,1,0:T(8,128)} async-done(((f32[2,1024,256]{2,1,0:T(8,128)}), f32[2,128,256]{2,1,0:T(8,128)}) %reduce-scatter.3.cloned.1.call-update) | async-done | bytes 262160 | tf_op jit(solution)/shard_map/reduce_scatter | solution.py:66
  247.0 1.7 fusion.36
  248.7 0.0 all-reduce.5.cloned.1.call-start
  248.8 25.6 %all-gather.8.cloned.1.call-done = bf16[2,1024,256]{2,1,0:T(8,128)(2,1)} async-done(((bf16[2,128,256]{2,1,0:T(8,128)(2,1)}), bf16[2,1024,256]{2,1,0:T(8,128)(2,1)}) %all-gather.8.cloned.1.call-update) | async-done | bytes 1048592 | tf_op jit(solution)/shard_map/all_gather | solution.py:38
  274.4 3.7 fusion.51
  278.1 0.8 fusion.43
  278.9 0.7 fusion.27
  279.7 1.5 copy-done.2
  281.1 2.9 fusion.16
  284.1 0.2 reduce-scatter.5.cloned.1.call-start
  284.3 102.8 %all-reduce.5.cloned.1.call-done = f32[2,2048,256]{2,1,0:T(8,128)} async-done(((f32[2,2048,256]{2,1,0:T(8,128)}), f32[2,2048,256]{2,1,0:T(8,128)}) %all-reduce.5.cloned.1.call-update) | async-done | bytes 4194320 | tf_op jit(solution)/shard_map/psum | solution.py:50
  387.1 6.2 %fusion.42 = (bf16[2,2048,256]{2,1,0:T(8,128)(2,1)S(1)}, f32[2,2048,256]{2,1,0:T(8,128)}) fusion(f32[2,2048,256]{2,1,0:T(8,128)} %all-reduce.5.cloned.1.call-done, f32[2,2048,256]{2,1,0:T(8,128)} %all-gather.6.cloned.1.call-done), kind=kLoop, calls=%fused_computation.58 | loop fusion | flops 2097152 | bytes 14680064 | tf_op jit(solution)/shard_map/convert_element_type | solution.py:52
  393.3 1.3 fusion.52
  394.5 1.0 copy.30
  395.5 0.8 fusion.40
  396.3 0.7 fusion.23
  397.0 1.5 copy-done.5
  398.5 2.8 fusion.8
  401.3 1.7 constant_dynamic-slice_fusion
  403.0 29.7 %reduce-scatter.5.cloned.1.call-done = f32[2,128,256]{2,1,0:T(8,128)} async-done(((f32[2,1024,256]{2,1,0:T(8,128)}), f32[2,128,256]{2,1,0:T(8,128)}) %reduce-scatter.5.cloned.1.call-update) | async-done | bytes 262160 | tf_op jit(solution)/shard_map/reduce_scatter | solution.py:66
  432.6 1.8 multiply_subtract_fusion
  (20 shorter events, 0.1 us)
Async XLA Ops:
  7.2 29.9 %all-gather.4.cloned.1.call-start = ((), (), s32[]{:S(2)}) async-start(), calls=%async_computation.2 | async-start | bytes 1179648 | tf_op jit(solution)/shard_map/all_gather | solution.py:38
  8.9 140.9 %all-reduce.3.cloned.1.call-start = ((), (), s32[]{:S(2)}) async-start(), calls=%async_computation.3 | async-start | bytes 8388608 | tf_op jit(solution)/shard_map/psum | solution.py:50
  16.4 7.4 %copy-start.8 = (s32[2,8,4]{1,2,0:T(4,128)S(1)}, s32[2,8,4]{1,2,0:T(4,128)}, u32[]{:S(2)}) copy-start(s32[2,8,4]{1,2,0:T(4,128)} %param.8) | copy-start | bytes 772
  41.6 2.2 copy-start
  46.7 156.7 %all-gather.6.cloned.1.call-start = ((), (), s32[]{:S(2)}) async-start(), calls=%async_computation.4 | async-start | bytes 4456448 | tf_op jit(solution)/shard_map/all_gather | solution.py:36
  47.5 199.6 %reduce-scatter.3.cloned.1.call-start = ((), (), s32[]{:S(2)}) async-start(), calls=%async_computation.5 | async-start | bytes 2359296 | tf_op jit(solution)/shard_map/reduce_scatter | solution.py:66
  203.4 4.6 %copy-start.1 = (bf16[2,8,256,4,128]{2,4,3,1,0:T(8,128)(2,1)S(1)}, bf16[2,8,256,4,128]{2,4,3,1,0:T(8,128)(2,1)}, u32[]{:S(2)}) copy-start(bf16[2,8,256,4,128]{2,4,3,1,0:T(8,128)(2,1)} %copy.11) | copy-start | bytes 12582916
  211.1 2.2 copy-start.4
  213.3 33.7 %copy-start.6 = (f32[2,128,256]{2,1,0:T(8,128)S(1)}, f32[2,128,256]{2,1,0:T(8,128)}, u32[]{:S(2)}) copy-start(f32[2,128,256]{2,1,0:T(8,128)} %param.9) | copy-start | bytes 786436
  213.3 33.7 %copy-start.9 = (f32[2]{0:T(128)S(1)}, f32[2]{0:T(128)}, u32[]{:S(2)}) copy-start(f32[2]{0:T(128)} %param.11) | copy-start | bytes 28
  216.1 58.3 %all-gather.8.cloned.1.call-start = ((), (), s32[]{:S(2)}) async-start(), calls=%async_computation.6 | async-start | bytes 1179648 | tf_op jit(solution)/shard_map/all_gather | solution.py:38
  248.7 138.3 %all-reduce.5.cloned.1.call-start = ((), (), s32[]{:S(2)}) async-start(), calls=%async_computation.7 | async-start | bytes 8388608 | tf_op jit(solution)/shard_map/psum | solution.py:50
  278.9 2.2 copy-start.2
  284.1 148.6 %reduce-scatter.5.cloned.1.call-start = ((), (), s32[]{:S(2)}) async-start(), calls=%async_computation.8 | async-start | bytes 2359296 | tf_op jit(solution)/shard_map/reduce_scatter | solution.py:66
  387.1 6.2 %copy-start.3 = (bf16[2,8,256,4,128]{2,4,3,1,0:T(8,128)(2,1)S(1)}, bf16[2,8,256,4,128]{2,4,3,1,0:T(8,128)(2,1)}, u32[]{:S(2)}) copy-start(bf16[2,8,256,4,128]{2,4,3,1,0:T(8,128)(2,1)} %copy.11) | copy-start | bytes 12582916
  396.3 2.2 copy-start.5
  398.5 34.1 %copy-start.7 = (f32[2,128,256]{2,1,0:T(8,128)S(1)}, f32[2,128,256]{2,1,0:T(8,128)}, u32[]{:S(2)}) copy-start(f32[2,128,256]{2,1,0:T(8,128)} %reduce-scatter.3.cloned.1.call-done) | copy-start | bytes 786436
Sparse Core Ops, SparseCore 0:
  10.2 26.7 all-gather.3
  46.8 102.8 all-reduce.2
  151.9 51.4 all-gather.5
  216.2 30.7 reduce-scatter.2
  249.1 25.2 all-gather.7
  284.2 102.8 all-reduce.4
  401.4 31.1 reduce-scatter.4
where the time goes:
time: 444 us; the launch traced here: 441 us
  waiting for transfers between devices  359 us (81%)
  local copies, waits for them, and re-layouts  24.7 us (6%)
  other arithmetic  21.6 us (5%)
  matrix products  21.4 us (5%)
  between operations  14.3 us (3%)
    psum x2, waiting for transfers between devices, local(): predicted = lax.psum(partial_value, 'col')  205 us
    reduce_scatter x2, waiting for transfers between devices, local(): lax.psum_scatter(gradient_part, 'row', scatter_dimension=1, tiled=True)  60.5 us
    all_gather x1, waiting for transfers between devices, local(): observed_block = lax.all_gather(observed, 'col', axis=1, tiled=True)  53.7 us
    all_gather x2, waiting for transfers between devices, local(): lax.all_gather(model.astype(jnp.bfloat16), 'row', axis=1, tiled=True)  38.9 us
    unnamed x22, local copies, waits for them, and re-layouts  21 us
    convert_element_type x2, other arithmetic, local(): misfit_half = full_misfit.astype(jnp.bfloat16)  10.5 us
    unnamed x4, matrix products  9.98 us
  transfers between devices with their start and end apart: 7, of which 7 were waited for; matrix products, arithmetic and copies ran while one was open for 4% of the time, Pallas kernels for 0%

commit v1 on v0

--- a/solution.py
+++ b/solution.py
@@ -33,7 +33,6 @@
     ).astype(jnp.float32)
     model = model_init
     misfit = model_init
-    observed_block = lax.all_gather(observed, "col", axis=1, tiled=True)
     for sweep in range(ITERS):
         gathered = lax.all_gather(model.astype(jnp.bfloat16), "row", axis=1, tiled=True)
         model_tiles = gathered.reshape(frequencies, cols_here, tile_size, 2 * right_count)
@@ -47,11 +46,13 @@
             "fiajk,fijkl->fial", u_factors, coefficient, preferred_element_type=jnp.float32
         )
         partial_value = partial_value.reshape(frequencies, rows_here * tile_size, 2 * right_count)
-        predicted = lax.psum(partial_value, "col")
-        full_misfit = predicted - observed_block
-        misfit_half = full_misfit.astype(jnp.bfloat16)
-        share = observed.shape[1]
-        misfit = lax.dynamic_slice_in_dim(full_misfit, lax.axis_index("col") * share, share, 1)
+        predicted = lax.psum_scatter(
+            partial_value.astype(jnp.bfloat16), "col", scatter_dimension=1, tiled=True
+        )
+        misfit = predicted.astype(jnp.float32) - observed
+        misfit_half = lax.all_gather(
+            misfit.astype(jnp.bfloat16), "col", axis=1, tiled=True
+        )
         misfit_tiles = misfit_half.reshape(frequencies, rows_here, tile_size, 2 * right_count)
         product = jnp.einsum(
             "fiajk,fial->fijkl", u_factors, misfit_tiles, preferred_element_type=jnp.float32
@@ -63,7 +64,9 @@
             "fiajk,fijkl->fjal", v_factors, back, preferred_element_type=jnp.float32
         )
         gradient_part = gradient_part.reshape(frequencies, cols_here * tile_size, 2 * right_count)
-        gradient = lax.psum_scatter(gradient_part, "row", scatter_dimension=1, tiled=True)
+        gradient = lax.psum_scatter(
+            gradient_part.astype(jnp.bfloat16), "row", scatter_dimension=1, tiled=True
+        ).astype(jnp.float32)
         model = model - step[:, None, None] * gradient
     return (model, misfit)
 

time: 444 us -> 418 us (0.941)
  waiting for transfers between devices: 359 us -> 337 us
  other arithmetic: 21.6 us -> 14.3 us
  matrix products: 21.4 us -> 26.2 us
    psum x2 -> x0, waiting for transfers between devices: 205 us -> none  [local(): predicted = lax.psum(partial_value, 'col')]
    reduce_scatter x2 -> x4, waiting for transfers between devices: 60.5 us -> 208 us  [the longest x2 147 us: local(): lax.psum_scatter(partial_value.astype(jnp.bfloat16), 'col', scatter_dimen...]
    all_gather x1 -> x2, waiting for transfers between devices: 53.7 us -> 90.7 us  [local(): lax.all_gather(misfit.astype(jnp.bfloat16), 'col', axis=1, tiled=True)]
    convert_element_type x2, other arithmetic: 10.5 us -> 3.26 us  [local(): misfit.astype(jnp.bfloat16)]
    unnamed x4, matrix products: 9.98 us -> 15.7 us
    unnamed x22 -> x20, local copies, waits for them, and re-layouts: 21 us -> 20.5 us
  transfers between devices with their start and end apart: 7 -> 8, of which waited for: 7 -> 8; matrix products, arithmetic and copies ran while one was open for 4% -> 4% of each run, Pallas kernels for 0% -> 0%
where the time goes in v1:
time: 418 us; the launch traced here: 415 us
  waiting for transfers between devices  337 us (81%)
  matrix products  26.2 us (6%)
  local copies, waits for them, and re-layouts  22.5 us (5%)
  other arithmetic  14.3 us (3%)
  between operations  14.3 us (3%)
    reduce_scatter x2, waiting for transfers between devices, local(): lax.psum_scatter(partial_value.astype(jnp.bfloat16), 'col', scatter_dimen...  147 us
    all_gather x2, waiting for transfers between devices, local(): lax.all_gather(misfit.astype(jnp.bfloat16), 'col', axis=1, tiled=True)  90.7 us
    reduce_scatter x2, waiting for transfers between devices, local(): lax.psum_scatter(gradient_part.astype(jnp.bfloat16), 'row', scatter_dimen...  61 us
    all_gather x2, waiting for transfers between devices, local(): lax.all_gather(model.astype(jnp.bfloat16), 'row', axis=1, tiled=True)  38.7 us
    unnamed x20, local copies, waits for them, and re-layouts  20.5 us
    unnamed x4, matrix products  15.7 us
  transfers between devices with their start and end apart: 8, of which 8 were waited for; matrix products, arithmetic and copies ran while one was open for 4% of the time, Pallas kernels for 0%

profile of v1, /device:TPU:1, one launch (start us, length us, event | category | flops | bytes accessed | tf_op | source)
XLA Modules:
  0.0 415.2 jit_solution(8225796991821594876)
XLA Ops:
  7.2 0.0 all-gather.5.cloned.1.call-start
  7.2 1.6 convert_element_type.71
  8.8 0.0 all-gather.5.cloned.1.call-update
  8.9 0.0 reduce-scatter.5.cloned.1.call-start
  8.9 7.4 %copy.11 = bf16[2,8,256,4,128]{2,4,3,1,0:T(8,128)(2,1)} copy(bf16[2,8,256,4,128]{4,3,2,1,0:T(4,128)(2,1)} %param.6) | data formatting | bytes 8388608 | tf_op args[0]
  16.3 7.5 %copy.8 = bf16[2,8,256,4,128]{2,4,1,3,0:T(8,128)(2,1)} copy(bf16[2,8,256,4,128]{4,3,2,1,0:T(4,128)(2,1)} %param.7) | data formatting | bytes 8388608 | tf_op args[1]
  23.8 0.1 fusion.45
  23.9 13.2 %all-gather.5.cloned.1.call-done = bf16[2,1024,256]{2,1,0:T(8,128)(2,1)} async-done(((bf16[2,128,256]{2,1,0:T(8,128)(2,1)}), bf16[2,1024,256]{2,1,0:T(8,128)(2,1)}) %all-gather.5.cloned.1.call-update) | async-done | bytes 1048592 | tf_op jit(solution)/shard_map/all_gather | solution.py:37
  37.1 3.7 fusion.57
  40.8 0.7 fusion.35
  41.5 0.8 fusion.55
  42.3 1.4 copy-done
  43.7 2.6 bitcast_convert_fusion.1
  46.4 0.0 reduce-scatter.5.cloned.1.call-update
  46.4 0.0 all-gather.7.cloned.1.call-start
  46.4 73.4 %reduce-scatter.5.cloned.1.call-done = bf16[2,128,256]{2,1,0:T(8,128)(2,1)} async-done(((bf16[2,2048,256]{2,1,0:T(8,128)(2,1)}), bf16[2,128,256]{2,1,0:T(8,128)(2,1)}) %reduce-scatter.5.cloned.1.call-update) | async-done | bytes 131088 | tf_op jit(solution)/shard_map/reduce_scatter | solution.py:49
  119.9 1.6 subtract_convert_fusion
  121.5 0.0 reduce-scatter.7.cloned.1.call-start
  121.5 45.5 %all-gather.7.cloned.1.call-done = bf16[2,2048,256]{2,1,0:T(8,128)(2,1)} async-done(((bf16[2,128,256]{2,1,0:T(8,128)(2,1)}), bf16[2,2048,256]{2,1,0:T(8,128)(2,1)}) %all-gather.7.cloned.1.call-update) | async-done | bytes 2097168 | tf_op jit(solution)/shard_map/all_gather | solution.py:53
  167.0 4.1 fusion.58
  171.1 1.0 copy.35
  172.1 0.7 fusion.31
  172.9 0.8 fusion.53
  173.7 1.4 copy-done.2
  175.1 2.6 bitcast_convert_fusion.3
  177.7 0.0 all-gather.9.cloned.1.call-start
  177.8 30.5 %reduce-scatter.7.cloned.1.call-done = bf16[2,128,256]{2,1,0:T(8,128)(2,1)} async-done(((bf16[2,1024,256]{2,1,0:T(8,128)(2,1)}), bf16[2,128,256]{2,1,0:T(8,128)(2,1)}) %reduce-scatter.7.cloned.1.call-update) | async-done | bytes 131088 | tf_op jit(solution)/shard_map/reduce_scatter | solution.py:67
  208.2 1.7 fusion.44
  209.9 0.0 reduce-scatter.9.cloned.1.call-start
  210.0 25.5 %all-gather.9.cloned.1.call-done = bf16[2,1024,256]{2,1,0:T(8,128)(2,1)} async-done(((bf16[2,128,256]{2,1,0:T(8,128)(2,1)}), bf16[2,1024,256]{2,1,0:T(8,128)(2,1)}) %all-gather.9.cloned.1.call-update) | async-done | bytes 1048592 | tf_op jit(solution)/shard_map/all_gather | solution.py:37
  235.5 3.7 fusion.59
  239.2 0.7 fusion.27
  239.9 0.8 fusion.51
  240.7 1.4 copy-done.1
  242.1 2.6 bitcast_convert_fusion
  244.8 0.0 all-gather.11.cloned.1.call-start
  244.8 73.4 %reduce-scatter.9.cloned.1.call-done = bf16[2,128,256]{2,1,0:T(8,128)(2,1)} async-done(((bf16[2,2048,256]{2,1,0:T(8,128)(2,1)}), bf16[2,128,256]{2,1,0:T(8,128)(2,1)}) %reduce-scatter.9.cloned.1.call-update) | async-done | bytes 131088 | tf_op jit(solution)/shard_map/reduce_scatter | solution.py:49
  318.2 1.7 fusion.50
  319.9 0.2 reduce-scatter.11.cloned.1.call-start
  320.2 45.2 %all-gather.11.cloned.1.call-done = bf16[2,2048,256]{2,1,0:T(8,128)(2,1)} async-done(((bf16[2,128,256]{2,1,0:T(8,128)(2,1)}), bf16[2,2048,256]{2,1,0:T(8,128)(2,1)}) %all-gather.11.cloned.1.call-update) | async-done | bytes 2097168 | tf_op jit(solution)/shard_map/all_gather | solution.py:53
  365.4 4.1 fusion.60
  369.5 1.0 copy.34
  370.5 0.7 fusion.23
  371.3 0.8 fusion.48
  372.0 1.4 copy-done.3
  373.4 2.6 bitcast_convert_fusion.2
  376.1 30.5 %reduce-scatter.11.cloned.1.call-done = bf16[2,128,256]{2,1,0:T(8,128)(2,1)} async-done(((bf16[2,1024,256]{2,1,0:T(8,128)(2,1)}), bf16[2,128,256]{2,1,0:T(8,128)(2,1)}) %reduce-scatter.11.cloned.1.call-update) | async-done | bytes 131088 | tf_op jit(solution)/shard_map/reduce_scatter | solution.py:67
  406.6 1.7 multiply_subtract_fusion
  (20 shorter events, 0.1 us)
Async XLA Ops:
  7.2 29.9 %all-gather.5.cloned.1.call-start = ((), (), s32[]{:S(2)}) async-start(), calls=%async_computation.4 | async-start | bytes 1179648 | tf_op jit(solution)/shard_map/all_gather | solution.py:37
  8.9 111.0 %reduce-scatter.5.cloned.1.call-start = ((), (), s32[]{:S(2)}) async-start(), calls=%async_computation.5 | async-start | bytes 2228224 | tf_op jit(solution)/shard_map/reduce_scatter | solution.py:49
  16.3 7.5 %copy-start.7 = (s32[2,8,4]{1,2,0:T(4,128)S(1)}, s32[2,8,4]{1,2,0:T(4,128)}, u32[]{:S(2)}) copy-start(s32[2,8,4]{1,2,0:T(4,128)} %param.8) | copy-start | bytes 772
  41.5 2.2 copy-start
  43.7 76.1 %copy-start.5 = (f32[2,128,256]{2,1,0:T(8,128)S(1)}, f32[2,128,256]{2,1,0:T(8,128)}, u32[]{:S(2)}) copy-start(f32[2,128,256]{2,1,0:T(8,128)} %param.10) | copy-start | bytes 786436
  46.4 120.6 %all-gather.7.cloned.1.call-start = ((), (), s32[]{:S(2)}) async-start(), calls=%async_computation.6 | async-start | bytes 2228224 | tf_op jit(solution)/shard_map/all_gather | solution.py:53
  121.5 86.7 %reduce-scatter.7.cloned.1.call-start = ((), (), s32[]{:S(2)}) async-start(), calls=%async_computation.7 | async-start | bytes 1179648 | tf_op jit(solution)/shard_map/reduce_scatter | solution.py:67
  172.9 2.2 copy-start.2
  175.1 33.2 %copy-start.4 = (f32[2,128,256]{2,1,0:T(8,128)S(1)}, f32[2,128,256]{2,1,0:T(8,128)}, u32[]{:S(2)}) copy-start(f32[2,128,256]{2,1,0:T(8,128)} %param.9) | copy-start | bytes 786436
  175.1 33.2 %copy-start.8 = (f32[2]{0:T(128)S(1)}, f32[2]{0:T(128)}, u32[]{:S(2)}) copy-start(f32[2]{0:T(128)} %param.11) | copy-start | bytes 28
  177.7 57.8 %all-gather.9.cloned.1.call-start = ((), (), s32[]{:S(2)}) async-start(), calls=%async_computation.8 | async-start | bytes 1179648 | tf_op jit(solution)/shard_map/all_gather | solution.py:37
  209.9 108.3 %reduce-scatter.9.cloned.1.call-start = ((), (), s32[]{:S(2)}) async-start(), calls=%async_computation.9 | async-start | bytes 2228224 | tf_op jit(solution)/shard_map/reduce_scatter | solution.py:49
  239.9 2.2 copy-start.1
  244.8 120.6 %all-gather.11.cloned.1.call-start = ((), (), s32[]{:S(2)}) async-start(), calls=%async_computation.10 | async-start | bytes 2228224 | tf_op jit(solution)/shard_map/all_gather | solution.py:53
  319.9 86.6 %reduce-scatter.11.cloned.1.call-start = ((), (), s32[]{:S(2)}) async-start(), calls=%async_computation.11 | async-start | bytes 1179648 | tf_op jit(solution)/shard_map/reduce_scatter | solution.py:67
  371.2 2.2 copy-start.3
  373.4 33.2 %copy-start.6 = (bf16[2,128,256]{2,1,0:T(8,128)(2,1)S(1)}, bf16[2,128,256]{2,1,0:T(8,128)(2,1)}, u32[]{:S(2)}) copy-start(bf16[2,128,256]{2,1,0:T(8,128)(2,1)} %reduce-scatter.7.cloned.1.call-done) | copy-start | bytes 393220
Sparse Core Ops, SparseCore 0:
  10.2 26.7 all-gather.4
  46.5 73.3 reduce-scatter.4
  122.6 44.3 all-gather.6
  177.8 30.3 reduce-scatter.6
  210.3 25.0 all-gather.8
  244.9 73.3 reduce-scatter.8
  321.0 44.3 all-gather.10
  376.2 30.3 reduce-scatter.10

commit v2 on v0

v2 whole, which is shorter than its diff:
```python
import functools

import jax
import jax.numpy as jnp
from jax import lax
from jax.experimental import pallas as pl
from jax.experimental.pallas import tpu as pltpu
from jax.sharding import PartitionSpec as P

ITERS = 2
MESH = pl.DeviceIdType.MESH
F32, BF16 = jnp.float32, jnp.bfloat16
LANES = 128
TRANS_B = (((1,), (1,)), ((), ()))


def kernel(
    u_hbm, v_hbm, ranks, model_in, observed, step,
    model_out, misfit_out,
    u_raw, v_raw, u_tiles, v_tiles, wide, expanded_f, expanded_b,
    model_t, observed_t, misfit_t,
    x_all, sum_a, sum_b, got_a, got_b, keep_a, keep_b, next_a, next_b, last_a, last_b,
    r_a, r_b, grad, grad_got, grad_keep, grad_send, grad_last,
    load_sem, send_sem, recv_sem,
):
    freqs, rows, cols = u_raw.shape[0], u_raw.shape[1], v_tiles.shape[1]
    tile = v_tiles.shape[2]
    half = tile // 2
    col, row = lax.axis_index("col"), lax.axis_index("row")
    y, z = col // 4, col % 4
    x, core = row // 2, row % 2

    def at_y(o):
        return ((y + o) % 4 * 4 + z, row)

    def at_z(o):
        return (y * 4 + (z + o) % 4, row)

    def at_x(o):
        return (col, (x + o) % 4 * 2 + core)

    partner = (col, x * 2 + 1 - core)
    numbers = {}

    def remote(name, src, dst, device):
        number = numbers.setdefault(name, len(numbers))
        return pltpu.make_async_remote_copy(
            src_ref=src, dst_ref=dst, send_sem=send_sem.at[number], recv_sem=recv_sem.at[number],
            device_id=device, device_id_type=MESH,
        )

    loads = {}
    for f in range(freqs):
        for n, (src, dst) in enumerate(((v_hbm, v_raw), (u_hbm, u_raw))):
            loads[f, n] = pltpu.make_async_copy(src.at[f], dst.at[f], load_sem.at[2 * f + n])
            loads[f, n].start()

    barrier = pltpu.get_barrier_semaphore()
    peers = [at_y(o) for o in (1, 2, 3)] + [at_z(o) for o in (1, 2, 3)] + [at_x(o) for o in (1, 2, 3)] + [partner]
    for peer in peers:
        pl.semaphore_signal(barrier, inc=1, device_id=peer, device_id_type=MESH)

    for f in range(freqs):
        turned = model_in[f].T
        model_t[f] = turned
        x_all[f, row] = turned.astype(BF16)
    pl.semaphore_wait(barrier, len(peers))

    lane = lax.broadcasted_iota(jnp.int32, (1, LANES), 1)
    sign = jnp.where(lane < LANES // 2, 1.0, -1.0).astype(F32)
    lane_k = lane % (LANES // 2)

    def relayout(f, raw, put):
        def one(i, carry):
            wide[...] = raw[f, i].astype(F32)
            for j in range(cols):
                piece = wide[pl.ds(j, tile, stride=cols), :]
                piece = jnp.where(lane_k < ranks[(f * rows + i) * cols + j], piece, 0.0)
                put(i, j, piece.astype(BF16))
            return carry

        lax.fori_loop(0, rows, one, 0)

    def relayout_v(f):
        loads[f, 0].wait()

        def put(i, j, piece):
            v_tiles[f, j, :, pl.ds(pl.multiple_of(i * LANES, LANES), LANES)] = piece

        relayout(f, v_raw, put)

    def relayout_u(f):
        loads[f, 1].wait()

        def put(i, j, piece):
            u_tiles[f, i, :, j * LANES:(j + 1) * LANES] = piece

        relayout(f, u_raw, put)

    def gather_x_copies(f):
        own = x_all.at[f, row]
        return [remote(("a", f, o), own, own, at_x(o)) for o in (1, 3, 2)] + [remote(("a", f, 0), own, own, partner)]

    def gather_x_pass(f):
        copies = []
        for o in (1, 3, 2):
            slot = x_all.at[f, (x - o + 4) % 4 * 2 + core]
            copies.append(remote(("ap", f, o), slot, slot, partner))
        return copies

    def gather_x_start(f):
        for copy in gather_x_copies(f):
            copy.start()

    def gather_x_mid(f):
        for copy, onward in zip(gather_x_copies(f)[:3], gather_x_pass(f)):
            copy.wait_recv()
            onward.start()

    def gather_x_end(f):
        copies = gather_x_copies(f)
        copies[3].wait_recv()
        for onward in gather_x_pass(f):
            onward.wait()
        for copy in copies:
            copy.wait_send()

    def expand(top, bottom):
        return (
            (top + sign * pltpu.roll(bottom, LANES // 2, 1)).astype(BF16),
            (bottom - sign * pltpu.roll(top, LANES // 2, 1)).astype(BF16),
        )

    def forward_products(f):
        def one(j, carry):
            left = jnp.concatenate([x_all[f, 2 * j], x_all[f, 2 * j + 1]], axis=1)
            product = jnp.dot(left, v_tiles[f, j], preferred_element_type=F32)
            for i in range(rows):
                part = product[:, i * LANES:(i + 1) * LANES]
                top, bottom = expand(part[:half], part[half:])
                at = pl.ds(pl.multiple_of(j * LANES, LANES), LANES)
                expanded_f[i, :half, at] = top
                expanded_f[i, half:, at] = bottom
            return carry

        lax.fori_loop(0, cols, one, 0)

    def forward_sums(f):
        def one(i, carry):
            total = lax.dot_general(expanded_f[i], u_tiles[f, i], TRANS_B, preferred_element_type=F32)
            total = total.astype(BF16)
            for h in range(2):
                part = total[:, h * LANES:(h + 1) * LANES]
                sum_a[f, 2 * i + h] = part[:half]
                sum_b[f, (2 * (i % 2) + h) * 4 + i // 2] = part[half:]
            return carry

        lax.fori_loop(0, rows, one, 0)

    def first_copies(f):
        copies = []
        for o in (2, 1, 3):
            copies.append(remote(("c1a", f, o), sum_a.at[f, pl.ds((y + o) % 4 * 4, 4)], got_a.at[f, o - 1], at_y(o)))
            copies.append(remote(("c1b", f, o), sum_b.at[f, pl.ds((z + o) % 4 * 4, 4)], got_b.at[f, o - 1], at_z(o)))
        return copies

    def second_copies(f):
        copies = []
        for o in (2, 1, 3):
            copies.append(remote(("c2a", f, o), next_a.at[f, (z + o) % 4], last_a.at[f, o - 1], at_z(o)))
            copies.append(remote(("c2b", f, o), next_b.at[f, (y + o) % 4], last_b.at[f, o - 1], at_y(o)))
        return copies

    def start(copies):
        for copy in copies:
            copy.start()

    def wait(copies):
        for copy in copies:
            copy.wait()

    def first_end(f):
        wait(first_copies(f))
        for q in range(4):
            for own, got, keep, onward, at in (
                (sum_a, got_a, keep_a, next_a, y), (sum_b, got_b, keep_b, next_b, z)
            ):
                total = own[f, at * 4 + q].astype(F32)
                for o in range(3):
                    total = total + got[f, o, q].astype(F32)
                keep[f, q] = total
                onward[f, q] = total.astype(BF16)
        start(second_copies(f))

    def gather_first(f):
        copies = []
        own_a, own_b = r_a.at[f, y * 4 + z], r_b.at[f, z * 4 + y]
        for o in (2, 1, 3):
            copies.append(remote(("e1a", f, o), own_a, own_a, at_z(o)))
            copies.append(remote(("e1b", f, o), own_b, own_b, at_y(o)))
        return copies

    def gather_second(f):
        copies = []
        own_a, own_b = r_a.at[f, pl.ds(y * 4, 4)], r_b.at[f, pl.ds(z * 4, 4)]
        for o in (2, 1, 3):
            copies.append(remote(("e2a", f, o), own_a, own_a, at_y(o)))
            copies.append(remote(("e2b", f, o), own_b, own_b, at_z(o)))
        return copies

    def second_end(f, last):
        wait(second_copies(f))
        for keep, got, to, rows_at, at, slot in (
            (keep_a, last_a, r_a, slice(0, half), z, y * 4 + z),
            (keep_b, last_b, r_b, slice(half, tile), y, z * 4 + y),
        ):
            total = keep[f, at]
            for o in range(3):
                total = total + got[f, o].astype(F32)
            total = total - observed_t[f, rows_at]
            if last:
                misfit_t[f, rows_at] = total
            to[f, slot] = total.astype(BF16)
        start(gather_first(f))

    def backward_products(f):
        def one(i, carry):
            left_a = jnp.concatenate([r_a[f, 2 * i], r_a[f, 2 * i + 1]], axis=1)
            at_b = 2 * (i % 2) * 4 + i // 2
            left_b = jnp.concatenate([r_b[f, at_b], r_b[f, at_b + 4]], axis=1)
            left = jnp.concatenate([left_a, left_b], axis=0)
            product = jnp.dot(left, u_tiles[f, i], preferred_element_type=F32)
            for j in range(cols):
                part = product[:, j * LANES:(j + 1) * LANES]
                top, bottom = expand(part[:half], part[half:])
                at = pl.ds(pl.multiple_of(i * LANES, LANES), LANES)
                expanded_b[j, :half, at] = top
                expanded_b[j, half:, at] = bottom
            return carry

        lax.fori_loop(0, rows, one, 0)

    def pair_copy(f, j):
        return remote(("g1", f, j), grad.at[f, 1 - core, j], grad_got.at[f, j], partner)

    def backward_sums(f):
        for j in range(cols):
            total = lax.dot_general(expanded_b[j], v_tiles[f, j], TRANS_B, preferred_element_type=F32)
            for h in range(2):
                grad[f, h, j] = total[:, h * LANES:(h + 1) * LANES]
            pair_copy(f, j).start()

    def across_copies(f):
        return [
            remote(("g2", f, o), grad_send.at[f, (x + o) % 4], grad_last.at[f, o - 1], at_x(o)) for o in (2, 1, 3)
        ]

    def pair_end(f):
        for j in range(cols):
            pair_copy(f, j).wait()
            total = grad[f, core, j] + grad_got[f, j]
            grad_keep[f, j] = total
            grad_send[f, j] = total.astype(BF16)
        start(across_copies(f))

    def across_end(f, last):
        wait(across_copies(f))
        total = grad_keep[f, x]
        for o in range(3):
            total = total + grad_last[f, o].astype(F32)
        new = model_t[f] - step[f] * total
        if last:
            model_out[f] = new.T
        else:
            model_t[f] = new
            x_all[f, row] = new.astype(BF16)

    for f in range(freqs):
        gather_x_start(f)
    relayout_v(0)
    gather_x_mid(0)
    relayout_u(0)
    for f in range(freqs):
        observed_t[f] = observed[f].T
    for sweep in range(ITERS):
        last = sweep == ITERS - 1
        gather_x_end(0)
        forward_products(0)
        gather_x_mid(1)
        forward_sums(0)
        start(first_copies(0))
        if sweep == 0:
            relayout_v(1)
            relayout_u(1)
        gather_x_end(1)
        forward_products(1)
        forward_sums(1)
        start(first_copies(1))
        for f in range(freqs):
            first_end(f)
        for f in range(freqs):
            second_end(f, last)
        for f in range(freqs):
            wait(gather_first(f))
            start(gather_second(f))
        if last:
            for f in range(freqs):
                misfit_out[f] = misfit_t[f].T
        wait(gather_second(0))
        backward_products(0)
        backward_sums(0)
        wait(gather_second(1))
        backward_products(1)
        pair_end(0)
        backward_sums(1)
        pair_end(1)
        for f in range(freqs):
            across_end(f, last)
            if not last:
                gather_x_start(f)
        if not last:
            gather_x_mid(0)


def local(u_factors, v_factors, ranks, model_init, observed, step):
    freqs, rows, tile, cols, width = u_factors.shape
    both, share = model_init.shape[2], model_init.shape[1]
    half = both // 2
    raw = (freqs, rows, tile * cols, width)
    vmem = lambda shape, kind: pltpu.VMEM(shape, kind)
    scratch = [
        vmem(raw, BF16), vmem(raw, BF16),
        vmem((freqs, rows, tile, cols * width), BF16), vmem((freqs, cols, tile, rows * width), BF16),
        vmem((tile * cols, width), F32),
        vmem((rows, both, cols * width), BF16), vmem((cols, both, rows * width), BF16),
        vmem((freqs, both, share), F32), vmem((freqs, both, share), F32), vmem((freqs, both, share), F32),
        vmem((freqs, 8, both, share), BF16),
        vmem((freqs, 16, half, share), BF16), vmem((freqs, 16, half, share), BF16),
        vmem((freqs, 3, 4, half, share), BF16), vmem((freqs, 3, 4, half, share), BF16),
        vmem((freqs, 4, half, share), F32), vmem((freqs, 4, half, share), F32),
        vmem((freqs, 4, half, share), BF16), vmem((freqs, 4, half, share), BF16),
        vmem((freqs, 3, half, share), BF16), vmem((freqs, 3, half, share), BF16),
        vmem((freqs, 16, half, share), BF16), vmem((freqs, 16, half, share), BF16),
        vmem((freqs, 2, cols, both, share), F32), vmem((freqs, cols, both, share), F32),
        vmem((freqs, cols, both, share), F32), vmem((freqs, cols, both, share), BF16),
        vmem((freqs, 3, both, share), BF16),
        pltpu.SemaphoreType.DMA((2 * freqs,)),
        pltpu.SemaphoreType.DMA((76,)), pltpu.SemaphoreType.DMA((76,)),
    ]
    in_vmem = pl.BlockSpec(memory_space=pltpu.VMEM)
    in_smem = pl.BlockSpec(memory_space=pltpu.SMEM)
    anywhere = pl.BlockSpec(memory_space=pl.ANY)
    return pl.pallas_call(
        kernel,
        out_shape=(
            jax.ShapeDtypeStruct(model_init.shape, F32), jax.ShapeDtypeStruct(observed.shape, F32),
        ),
        in_specs=[anywhere, anywhere, in_smem, in_vmem, in_vmem, in_smem],
        out_specs=(in_vmem, in_vmem),
        scratch_shapes=scratch,
        compiler_params=pltpu.CompilerParams(
            collective_id=0, has_side_effects=True, vmem_limit_bytes=60 * 2**20
        ),
    )(u_factors.reshape(raw), v_factors.reshape(raw), ranks.reshape(-1), model_init, observed, step)


def solution(mesh):
    return jax.shard_map(
        local,
        mesh=mesh,
        in_specs=(
            P(None, "row", None, "col", None),
            P(None, "row", None, "col", None),
            P(None, "row", "col"),
            P(None, ("col", "row"), None),
            P(None, ("row", "col"), None),
            P(),
        ),
        out_specs=(P(None, ("col", "row"), None), P(None, ("row", "col"), None)),
        check_vma=False,
    )
```

time: 444 us -> 130 us (0.29)
  waiting for transfers between devices: 359 us -> 0 us
  Pallas kernels: 0 us -> 124 us
  other arithmetic: 21.6 us -> 0 us
  matrix products: 21.4 us -> 0 us
  local copies, waits for them, and re-layouts: 24.7 us -> 4.71 us
  between operations: 14.3 us -> 0.64 us
    psum x2 -> x0, waiting for transfers between devices: 205 us -> none  [local(): predicted = lax.psum(partial_value, 'col')]
    pallas_call x0 -> x1, Pallas kernels: none -> 124 us  [local(): pl.pallas_call(kernel, out_shape=(jax.ShapeDtypeStruct(model_init.shape,...]
    all_gather x3 -> x0, waiting for transfers between devices: 92.6 us -> none  [the longest x1 53.7 us: local(): observed_block = lax.all_gather(observed, 'col', axis=1, tiled=True)]
    reduce_scatter x2 -> x0, waiting for transfers between devices: 60.5 us -> none  [local(): lax.psum_scatter(gradient_part, 'row', scatter_dimension=1, tiled=True)]
    unnamed x22 -> x3, local copies, waits for them, and re-layouts: 21 us -> 4.11 us
    convert_element_type x5 -> x0, other arithmetic: 13.9 us -> none  [the longest x2 10.5 us: local(): misfit_half = full_misfit.astype(jnp.bfloat16)]
    dot_general x4 -> x0, matrix products: 11.4 us -> none  [the longest x2 5.83 us: local(): jnp.einsum('fiajk,fijkl->fial', u_factors, coefficient, preferred_element...]
    unnamed x4 -> x0, matrix products: 9.98 us -> none
  transfers between devices with their start and end apart: 7 -> 0, of which waited for: 7 -> 0; matrix products, arithmetic and copies ran while one was open for 4% -> 0% of each run, Pallas kernels for 0% -> 0%
where the time goes in v2:
time: 130 us; the launch traced here: 129 us
  Pallas kernels  124 us (95%)
  local copies, waits for them, and re-layouts  4.71 us (4%)
    pallas_call x1, Pallas kernels, local(): pl.pallas_call(kernel, out_shape=(jax.ShapeDtypeStruct(model_init.shape,...  124 us
    unnamed x3, local copies, waits for them, and re-layouts  4.11 us

profile of v2, /device:TPU:1, one launch (start us, length us, event | category | flops | bytes accessed | tf_op | source)
XLA Modules:
  0.0 129.3 jit_solution(8488472185059159519)
XLA Ops:
  0.6 0.8 copy.9
  1.4 0.6 reshape.15.ranks
  2.0 124.0 %shard_map.77 = (f32[2,128,256]{2,1,0:T(8,128)}, f32[2,128,256]{2,1,0:T(8,128)}) custom-call(bf16[2,8,1024,128]{3,2,1,0:T(8,128)(2,1)} %bitcast.2, bf16[2,8,1024,128]{3,2,1,0:T(8,128)(2,1)} %bitcast.3, s32[64]{0:T(128)} %reshape.15.ranks, f32[2,128,256]{2,1,0:T(8,128)} %model_in.1, f32[2,128,256]{2,1,0:T(8,128)} %observed.1, f32[2]{0:T(128)} %step.1), custom_call_target="tpu_custom_call" | custom-call | tf_op jit(solution)/shard_map/pallas_call | solution.py:353
  126.0 1.7 %copy.12 = f32[2,128,256]{2,1,0:T(8,128)} copy(f32[2,128,256]{2,1,0:T(8,128)} %get-tuple-element.4) | data formatting | bytes 524288
  127.6 1.7 %copy.13 = f32[2,128,256]{2,1,0:T(8,128)} copy(f32[2,128,256]{2,1,0:T(8,128)} %get-tuple-element.5) | data formatting | bytes 524288

commit v3 on v2

--- a/solution.py
+++ b/solution.py
@@ -24,8 +24,8 @@
     load_sem, send_sem, recv_sem,
 ):
     freqs, rows, cols = u_raw.shape[0], u_raw.shape[1], v_tiles.shape[1]
-    tile = v_tiles.shape[2]
-    half = tile // 2
+    tile = v_tiles.shape[2] // 2
+    half = x_all.shape[2] // 2
     col, row = lax.axis_index("col"), lax.axis_index("row")
     y, z = col // 4, col % 4
     x, core = row // 2, row % 2
@@ -67,35 +67,56 @@
     pl.semaphore_wait(barrier, len(peers))
 
     lane = lax.broadcasted_iota(jnp.int32, (1, LANES), 1)
-    sign = jnp.where(lane < LANES // 2, 1.0, -1.0).astype(F32)
+    low = lane < LANES // 2
     lane_k = lane % (LANES // 2)
 
-    def relayout(f, raw, put):
-        def one(i, carry):
-            wide[...] = raw[f, i].astype(F32)
-            for j in range(cols):
-                piece = wide[pl.ds(j, tile, stride=cols), :]
-                piece = jnp.where(lane_k < ranks[(f * rows + i) * cols + j], piece, 0.0)
-                put(i, j, piece.astype(BF16))
-            return carry
-
-        lax.fori_loop(0, rows, one, 0)
+    def pick(first, second):
+        return jnp.where(low, first, second)
+
+    def swap(value):
+        return pltpu.roll(value, LANES // 2, 1)
+
+    def planes(f, raw, p):
+        found = []
+        for e in range(2):
+            wide[e] = raw[f, 2 * p + e].astype(F32)
+        for j in range(cols):
+            pair = []
+            for e in range(2):
+                piece = wide[e, pl.ds(j, tile, stride=cols), :]
+                pair.append(jnp.where(lane_k < ranks[f, j, 2 * p + e], piece, 0.0))
+            found.append(pair)
+        return found
+
+    def joined(first, second):
+        return pick(first, swap(second)).astype(BF16), pick(swap(first), second).astype(BF16)
 
     def relayout_v(f):
         loads[f, 0].wait()
 
-        def put(i, j, piece):
-            v_tiles[f, j, :, pl.ds(pl.multiple_of(i * LANES, LANES), LANES)] = piece
-
-        relayout(f, v_raw, put)
+        def one(p, carry):
+            at = pl.ds(pl.multiple_of(p * LANES, LANES), LANES)
+            for j, pair in enumerate(planes(f, v_raw, p)):
+                real, imaginary = joined(pair[j % 2], pair[1 - j % 2])
+                v_tiles[f, j, :tile, at] = real
+                v_tiles[f, j, tile:, at] = imaginary
+            return carry
+
+        lax.fori_loop(0, rows // 2, one, 0)
 
     def relayout_u(f):
         loads[f, 1].wait()
 
-        def put(i, j, piece):
-            u_tiles[f, i, :, j * LANES:(j + 1) * LANES] = piece
-
-        relayout(f, u_raw, put)
+        def one(p, carry):
+            found = planes(f, u_raw, p)
+            for e in range(2):
+                for jp in range(cols // 2):
+                    real, imaginary = joined(found[2 * jp + e][e], found[2 * jp + 1 - e][e])
+                    u_tiles[f, 2 * p + e, :tile, jp * LANES:(jp + 1) * LANES] = real
+                    u_tiles[f, 2 * p + e, tile:, jp * LANES:(jp + 1) * LANES] = imaginary
+            return carry
+
+        lax.fori_loop(0, rows // 2, one, 0)
 
     def gather_x_copies(f):
         own = x_all.at[f, row]
@@ -125,29 +146,40 @@
         for copy in copies:
             copy.wait_send()
 
-    def expand(top, bottom):
-        return (
-            (top + sign * pltpu.roll(bottom, LANES // 2, 1)).astype(BF16),
-            (bottom - sign * pltpu.roll(top, LANES // 2, 1)).astype(BF16),
-        )
+    def adjoint_left(value):
+        return jnp.concatenate([value, jnp.concatenate([value[half:], -value[:half]], axis=0)], axis=1)
+
+    def turned_left(value):
+        return jnp.concatenate([-value[half:], value[:half]], axis=0)
 
     def forward_products(f):
-        def one(j, carry):
-            left = jnp.concatenate([x_all[f, 2 * j], x_all[f, 2 * j + 1]], axis=1)
-            product = jnp.dot(left, v_tiles[f, j], preferred_element_type=F32)
-            for i in range(rows):
-                part = product[:, i * LANES:(i + 1) * LANES]
-                top, bottom = expand(part[:half], part[half:])
-                at = pl.ds(pl.multiple_of(j * LANES, LANES), LANES)
-                expanded_f[i, :half, at] = top
-                expanded_f[i, half:, at] = bottom
+        def one(jp, carry):
+            lefts = []
+            for e in range(2):
+                at = 2 * (2 * jp + e)
+                lefts.append(adjoint_left(jnp.concatenate([x_all[f, at], x_all[f, at + 1]], axis=1)))
+            at = pl.ds(pl.multiple_of(jp * LANES, LANES), LANES)
+            for q in range(rows // 4):
+                even, odd = (
+                    jnp.dot(lefts[e], v_tiles[f, 2 * jp + e, :, q * tile:(q + 1) * tile], preferred_element_type=F32)
+                    for e in range(2)
+                )
+                for p in range(2):
+                    one_even, one_odd = even[:, p * LANES:(p + 1) * LANES], odd[:, p * LANES:(p + 1) * LANES]
+                    i = 4 * q + 2 * p
+                    expanded_f[i, :, at] = pick(one_even, one_odd).astype(BF16)
+                    expanded_f[i + 1, :, at] = pick(one_odd, one_even).astype(BF16)
             return carry
 
-        lax.fori_loop(0, cols, one, 0)
+        lax.fori_loop(0, cols // 2, one, 0)
 
     def forward_sums(f):
         def one(i, carry):
-            total = lax.dot_general(expanded_f[i], u_tiles[f, i], TRANS_B, preferred_element_type=F32)
+            left = expanded_f[i]
+            total = lax.dot_general(left, u_tiles[f, i, :tile], TRANS_B, preferred_element_type=F32)
+            total = total + lax.dot_general(
+                turned_left(left), u_tiles[f, i, tile:], TRANS_B, preferred_element_type=F32
+            )
             total = total.astype(BF16)
             for h in range(2):
                 part = total[:, h * LANES:(h + 1) * LANES]
@@ -224,28 +256,33 @@
         start(gather_first(f))
 
     def backward_products(f):
-        def one(i, carry):
-            left_a = jnp.concatenate([r_a[f, 2 * i], r_a[f, 2 * i + 1]], axis=1)
-            at_b = 2 * (i % 2) * 4 + i // 2
-            left_b = jnp.concatenate([r_b[f, at_b], r_b[f, at_b + 4]], axis=1)
-            left = jnp.concatenate([left_a, left_b], axis=0)
-            product = jnp.dot(left, u_tiles[f, i], preferred_element_type=F32)
-            for j in range(cols):
-                part = product[:, j * LANES:(j + 1) * LANES]
-                top, bottom = expand(part[:half], part[half:])
-                at = pl.ds(pl.multiple_of(i * LANES, LANES), LANES)
-                expanded_b[j, :half, at] = top
-                expanded_b[j, half:, at] = bottom
+        def one(p, carry):
+            found = []
+            for e in range(2):
+                i = 2 * p + e
+                left_a = jnp.concatenate([r_a[f, 2 * i], r_a[f, 2 * i + 1]], axis=1)
+                left_b = jnp.concatenate([r_b[f, 8 * e + p], r_b[f, 8 * e + 4 + p]], axis=1)
+                left = adjoint_left(jnp.concatenate([left_a, left_b], axis=0))
+                found.append(jnp.dot(left, u_tiles[f, i], preferred_element_type=F32))
+            at = pl.ds(pl.multiple_of(p * LANES, LANES), LANES)
+            for jp in range(cols // 2):
+                even, odd = (value[:, jp * LANES:(jp + 1) * LANES] for value in found)
+                expanded_b[2 * jp, :, at] = pick(even, odd).astype(BF16)
+                expanded_b[2 * jp + 1, :, at] = pick(odd, even).astype(BF16)
             return carry
 
-        lax.fori_loop(0, rows, one, 0)
+        lax.fori_loop(0, rows // 2, one, 0)
 
     def pair_copy(f, j):
         return remote(("g1", f, j), grad.at[f, 1 - core, j], grad_got.at[f, j], partner)
 
     def backward_sums(f):
         for j in range(cols):
-            total = lax.dot_general(expanded_b[j], v_tiles[f, j], TRANS_B, preferred_element_type=F32)
+            left = expanded_b[j]
+            total = lax.dot_general(left, v_tiles[f, j, :tile], TRANS_B, preferred_element_type=F32)
+            total = total + lax.dot_general(
+                turned_left(left), v_tiles[f, j, tile:], TRANS_B, preferred_element_type=F32
+            )
             for h in range(2):
                 grad[f, h, j] = total[:, h * LANES:(h + 1) * LANES]
             pair_copy(f, j).start()
@@ -330,9 +367,9 @@
     vmem = lambda shape, kind: pltpu.VMEM(shape, kind)
     scratch = [
         vmem(raw, BF16), vmem(raw, BF16),
-        vmem((freqs, rows, tile, cols * width), BF16), vmem((freqs, cols, tile, rows * width), BF16),
-        vmem((tile * cols, width), F32),
-        vmem((rows, both, cols * width), BF16), vmem((cols, both, rows * width), BF16),
+        vmem((freqs, rows, 2 * tile, cols * width // 2), BF16), vmem((freqs, cols, 2 * tile, rows * width // 2), BF16),
+        vmem((2, tile * cols, width), F32),
+        vmem((rows, both, cols * width // 2), BF16), vmem((cols, both, rows * width // 2), BF16),
         vmem((freqs, both, share), F32), vmem((freqs, both, share), F32), vmem((freqs, both, share), F32),
         vmem((freqs, 8, both, share), BF16),
         vmem((freqs, 16, half, share), BF16), vmem((freqs, 16, half, share), BF16),
@@ -359,9 +396,9 @@
         out_specs=(in_vmem, in_vmem),
         scratch_shapes=scratch,
         compiler_params=pltpu.CompilerParams(
-            collective_id=0, has_side_effects=True, vmem_limit_bytes=60 * 2**20
+            collective_id=0, has_side_effects=True, vmem_limit_bytes=52 * 2**20
         ),
-    )(u_factors.reshape(raw), v_factors.reshape(raw), ranks.reshape(-1), model_init, observed, step)
+    )(u_factors.reshape(raw), v_factors.reshape(raw), ranks.transpose(0, 2, 1), model_init, observed, step)
 
 
 def solution(mesh):

time: 130 us -> 119 us (0.915)
  Pallas kernels: 124 us -> 114 us
    pallas_call x1, Pallas kernels: 124 us -> 114 us  [local(): pl.pallas_call(kernel, out_shape=(jax.ShapeDtypeStruct(model_init.shape,...]
    unnamed x3 -> x10, local copies, waits for them, and re-layouts: 4.11 us -> 4.64 us
where the time goes in v3:
time: 119 us
  Pallas kernels  114 us (96%)
  local copies, waits for them, and re-layouts  4.64 us (4%)
    pallas_call x1, Pallas kernels, local(): pl.pallas_call(kernel, out_shape=(jax.ShapeDtypeStruct(model_init.shape,...  114 us
    unnamed x10, local copies, waits for them, and re-layouts  4.64 us

profile of v3, /device:TPU:1, one launch (start us, length us, event | category | flops | bytes accessed | tf_op | source)
XLA Modules:
  0.0 119.0 jit_solution(14256716709013619244)
XLA Ops:
  0.6 0.0 copy-start
  0.6 0.9 copy-done
  1.6 0.0 copy-start.1
  1.6 0.9 copy-done.1
  2.5 0.0 copy-start.2
  2.5 0.7 copy-done.2
  3.2 0.0 copy-start.3
  3.2 0.7 copy-done.3
  3.9 113.7 %shard_map.77 = (f32[2,128,256]{2,1,0:T(8,128)S(1)}, f32[2,128,256]{2,1,0:T(8,128)S(1)}) custom-call(bf16[2,8,1024,128]{3,2,1,0:T(8,128)(2,1)} %bitcast.4, bf16[2,8,1024,128]{3,2,1,0:T(8,128)(2,1)} %bitcast.5, s32[2,4,8]{2,1,0:T(4,128)S(1)} %bitcast.3, f32[2,128,256]{2,1,0:T(8,128)S(1)} %copy-done, f32[2,128,256]{2,1,0:T(8,128)S(1)} %copy-done.1, f32[2]{0:T(128)S(1)} %copy-done.3), custom_call_target="tpu_custom_call" | custom-call | tf_op jit(solution)/shard_map/pallas_call | solution.py:390
  117.6 0.7 copy.10
  118.3 0.7 copy.11
Async XLA Ops:
  0.6 1.0 copy-start
  1.6 0.9 copy-start.1
  2.5 0.7 copy-start.2
  3.2 0.7 copy-start.3

commit v4 on v3

--- a/solution.py
+++ b/solution.py
@@ -12,6 +12,13 @@
 F32, BF16 = jnp.float32, jnp.bfloat16
 LANES = 128
 TRANS_B = (((1,), (1,)), ((), ()))
+SPLIT = 2
+ORDER = (
+    0, 1, 2, 3, 0, 1, 0, 1, 2, 3, 2, 3, 0, 1, 2, 3, 0,
+    1, 2, 3, 0, 1, 2, 3, 0, 1, 0, 2, 1, 3, 0, 2, 1, 3,
+    0, 2, 0, 1, 3, 1, 2, 2, 0, 3, 3, 1, 2, 0, 3, 1, 2,
+    0, 3, 1, 2, 0, 3, 0, 1, 2, 1, 0, 3, 2, 1, 3, 2, 3,
+)
 
 
 def kernel(
@@ -24,6 +31,7 @@
     load_sem, send_sem, recv_sem,
 ):
     freqs, rows, cols = u_raw.shape[0], u_raw.shape[1], v_tiles.shape[1]
+    chains = freqs * SPLIT
     tile = v_tiles.shape[2] // 2
     half = x_all.shape[2] // 2
     col, row = lax.axis_index("col"), lax.axis_index("row")
@@ -60,10 +68,21 @@
     for peer in peers:
         pl.semaphore_signal(barrier, inc=1, device_id=peer, device_id_type=MESH)
 
+    def chain_rows(f, turned):
+        full = turned.shape[0] // 2
+        return [
+            (SPLIT * f + h, jnp.concatenate([turned[b + h * half:b + (h + 1) * half] for b in (0, full)], axis=0))
+            for h in range(SPLIT)
+        ]
+
+    def whole_rows(f, ref):
+        parts = [ref[SPLIT * f + h] for h in range(SPLIT)]
+        return jnp.concatenate([part[:half] for part in parts] + [part[half:] for part in parts], axis=0).T
+
     for f in range(freqs):
-        turned = model_in[f].T
-        model_t[f] = turned
-        x_all[f, row] = turned.astype(BF16)
+        for c, turned in chain_rows(f, model_in[f].T):
+            model_t[c] = turned
+            x_all[c, row] = turned.astype(BF16)
     pl.semaphore_wait(barrier, len(peers))
 
     lane = lax.broadcasted_iota(jnp.int32, (1, LANES), 1)
@@ -153,41 +172,37 @@
         return jnp.concatenate([-value[half:], value[:half]], axis=0)
 
     def forward_products(f):
-        def one(jp, carry):
+        for jp in range(cols // 2):
             lefts = []
             for e in range(2):
                 at = 2 * (2 * jp + e)
                 lefts.append(adjoint_left(jnp.concatenate([x_all[f, at], x_all[f, at + 1]], axis=1)))
-            at = pl.ds(pl.multiple_of(jp * LANES, LANES), LANES)
             for q in range(rows // 4):
                 even, odd = (
-                    jnp.dot(lefts[e], v_tiles[f, 2 * jp + e, :, q * tile:(q + 1) * tile], preferred_element_type=F32)
+                    jnp.dot(
+                        lefts[e], v_tiles[f // SPLIT, 2 * jp + e, :, q * tile:(q + 1) * tile],
+                        preferred_element_type=F32,
+                    )
                     for e in range(2)
                 )
                 for p in range(2):
                     one_even, one_odd = even[:, p * LANES:(p + 1) * LANES], odd[:, p * LANES:(p + 1) * LANES]
                     i = 4 * q + 2 * p
-                    expanded_f[i, :, at] = pick(one_even, one_odd).astype(BF16)
-                    expanded_f[i + 1, :, at] = pick(one_odd, one_even).astype(BF16)
-            return carry
-
-        lax.fori_loop(0, cols // 2, one, 0)
+                    expanded_f[i, :, jp * LANES:(jp + 1) * LANES] = pick(one_even, one_odd).astype(BF16)
+                    expanded_f[i + 1, :, jp * LANES:(jp + 1) * LANES] = pick(one_odd, one_even).astype(BF16)
 
     def forward_sums(f):
-        def one(i, carry):
+        for i in range(rows):
             left = expanded_f[i]
-            total = lax.dot_general(left, u_tiles[f, i, :tile], TRANS_B, preferred_element_type=F32)
+            total = lax.dot_general(left, u_tiles[f // SPLIT, i, :tile], TRANS_B, preferred_element_type=F32)
             total = total + lax.dot_general(
-                turned_left(left), u_tiles[f, i, tile:], TRANS_B, preferred_element_type=F32
+                turned_left(left), u_tiles[f // SPLIT, i, tile:], TRANS_B, preferred_element_type=F32
             )
             total = total.astype(BF16)
             for h in range(2):
                 part = total[:, h * LANES:(h + 1) * LANES]
                 sum_a[f, 2 * i + h] = part[:half]
                 sum_b[f, (2 * (i % 2) + h) * 4 + i // 2] = part[half:]
-            return carry
-
-        lax.fori_loop(0, rows, one, 0)
 
     def first_copies(f):
         copies = []
@@ -256,22 +271,18 @@
         start(gather_first(f))
 
     def backward_products(f):
-        def one(p, carry):
+        for p in range(rows // 2):
             found = []
             for e in range(2):
                 i = 2 * p + e
                 left_a = jnp.concatenate([r_a[f, 2 * i], r_a[f, 2 * i + 1]], axis=1)
                 left_b = jnp.concatenate([r_b[f, 8 * e + p], r_b[f, 8 * e + 4 + p]], axis=1)
                 left = adjoint_left(jnp.concatenate([left_a, left_b], axis=0))
-                found.append(jnp.dot(left, u_tiles[f, i], preferred_element_type=F32))
-            at = pl.ds(pl.multiple_of(p * LANES, LANES), LANES)
+                found.append(jnp.dot(left, u_tiles[f // SPLIT, i], preferred_element_type=F32))
             for jp in range(cols // 2):
                 even, odd = (value[:, jp * LANES:(jp + 1) * LANES] for value in found)
-                expanded_b[2 * jp, :, at] = pick(even, odd).astype(BF16)
-                expanded_b[2 * jp + 1, :, at] = pick(odd, even).astype(BF16)
-            return carry
-
-        lax.fori_loop(0, rows // 2, one, 0)
+                expanded_b[2 * jp, :, p * LANES:(p + 1) * LANES] = pick(even, odd).astype(BF16)
+                expanded_b[2 * jp + 1, :, p * LANES:(p + 1) * LANES] = pick(odd, even).astype(BF16)
 
     def pair_copy(f, j):
         return remote(("g1", f, j), grad.at[f, 1 - core, j], grad_got.at[f, j], partner)
@@ -279,9 +290,9 @@
     def backward_sums(f):
         for j in range(cols):
             left = expanded_b[j]
-            total = lax.dot_general(left, v_tiles[f, j, :tile], TRANS_B, preferred_element_type=F32)
+            total = lax.dot_general(left, v_tiles[f // SPLIT, j, :tile], TRANS_B, preferred_element_type=F32)
             total = total + lax.dot_general(
-                turned_left(left), v_tiles[f, j, tile:], TRANS_B, preferred_element_type=F32
+                turned_left(left), v_tiles[f // SPLIT, j, tile:], TRANS_B, preferred_element_type=F32
             )
             for h in range(2):
                 grad[f, h, j] = total[:, h * LANES:(h + 1) * LANES]
@@ -305,84 +316,79 @@
         total = grad_keep[f, x]
         for o in range(3):
             total = total + grad_last[f, o].astype(F32)
-        new = model_t[f] - step[f] * total
-        if last:
-            model_out[f] = new.T
-        else:
-            model_t[f] = new
+        new = model_t[f] - step[f // SPLIT] * total
+        model_t[f] = new
+        if not last:
             x_all[f, row] = new.astype(BF16)
-
-    for f in range(freqs):
+            gather_x_start(f)
+
+    def stages(f):
         gather_x_start(f)
-    relayout_v(0)
-    gather_x_mid(0)
-    relayout_u(0)
-    for f in range(freqs):
-        observed_t[f] = observed[f].T
-    for sweep in range(ITERS):
-        last = sweep == ITERS - 1
-        gather_x_end(0)
-        forward_products(0)
-        gather_x_mid(1)
-        forward_sums(0)
-        start(first_copies(0))
-        if sweep == 0:
-            relayout_v(1)
-            relayout_u(1)
-        gather_x_end(1)
-        forward_products(1)
-        forward_sums(1)
-        start(first_copies(1))
-        for f in range(freqs):
+        yield
+        for sweep in range(ITERS):
+            last = sweep == ITERS - 1
+            gather_x_mid(f)
+            yield
+            if sweep == 0 and f % SPLIT == 0:
+                relayout_v(f // SPLIT)
+                relayout_u(f // SPLIT)
+                for c, turned in chain_rows(f // SPLIT, observed[f // SPLIT].T):
+                    observed_t[c] = turned
+            gather_x_end(f)
+            forward_products(f)
+            forward_sums(f)
+            start(first_copies(f))
+            yield
             first_end(f)
-        for f in range(freqs):
+            yield
             second_end(f, last)
-        for f in range(freqs):
+            yield
             wait(gather_first(f))
             start(gather_second(f))
-        if last:
-            for f in range(freqs):
-                misfit_out[f] = misfit_t[f].T
-        wait(gather_second(0))
-        backward_products(0)
-        backward_sums(0)
-        wait(gather_second(1))
-        backward_products(1)
-        pair_end(0)
-        backward_sums(1)
-        pair_end(1)
-        for f in range(freqs):
+            if last and f % SPLIT == SPLIT - 1:
+                misfit_out[f // SPLIT] = whole_rows(f // SPLIT, misfit_t)
+            yield
+            wait(gather_second(f))
+            backward_products(f)
+            backward_sums(f)
+            yield
+            pair_end(f)
+            yield
             across_end(f, last)
-            if not last:
-                gather_x_start(f)
-        if not last:
-            gather_x_mid(0)
+            if last and f % SPLIT == SPLIT - 1:
+                model_out[f // SPLIT] = whole_rows(f // SPLIT, model_t)
+            yield
+
+    running = [stages(f) for f in range(chains)]
+    for f in ORDER:
+        next(running[f])
 
 
 def local(u_factors, v_factors, ranks, model_init, observed, step):
     freqs, rows, tile, cols, width = u_factors.shape
     both, share = model_init.shape[2], model_init.shape[1]
-    half = both // 2
+    chains, part = freqs * SPLIT, both // SPLIT
+    half = part // 2
     raw = (freqs, rows, tile * cols, width)
     vmem = lambda shape, kind: pltpu.VMEM(shape, kind)
     scratch = [
         vmem(raw, BF16), vmem(raw, BF16),
         vmem((freqs, rows, 2 * tile, cols * width // 2), BF16), vmem((freqs, cols, 2 * tile, rows * width // 2), BF16),
         vmem((2, tile * cols, width), F32),
-        vmem((rows, both, cols * width // 2), BF16), vmem((cols, both, rows * width // 2), BF16),
-        vmem((freqs, both, share), F32), vmem((freqs, both, share), F32), vmem((freqs, both, share), F32),
-        vmem((freqs, 8, both, share), BF16),
-        vmem((freqs, 16, half, share), BF16), vmem((freqs, 16, half, share), BF16),
-        vmem((freqs, 3, 4, half, share), BF16), vmem((freqs, 3, 4, half, share), BF16),
-        vmem((freqs, 4, half, share), F32), vmem((freqs, 4, half, share), F32),
-        vmem((freqs, 4, half, share), BF16), vmem((freqs, 4, half, share), BF16),
-        vmem((freqs, 3, half, share), BF16), vmem((freqs, 3, half, share), BF16),
-        vmem((freqs, 16, half, share), BF16), vmem((freqs, 16, half, share), BF16),
-        vmem((freqs, 2, cols, both, share), F32), vmem((freqs, cols, both, share), F32),
-        vmem((freqs, cols, both, share), F32), vmem((freqs, cols, both, share), BF16),
-        vmem((freqs, 3, both, share), BF16),
+        vmem((rows, part, cols * width // 2), BF16), vmem((cols, part, rows * width // 2), BF16),
+        vmem((chains, part, share), F32), vmem((chains, part, share), F32), vmem((chains, part, share), F32),
+        vmem((chains, 8, part, share), BF16),
+        vmem((chains, 16, half, share), BF16), vmem((chains, 16, half, share), BF16),
+        vmem((chains, 3, 4, half, share), BF16), vmem((chains, 3, 4, half, share), BF16),
+        vmem((chains, 4, half, share), F32), vmem((chains, 4, half, share), F32),
+        vmem((chains, 4, half, share), BF16), vmem((chains, 4, half, share), BF16),
+        vmem((chains, 3, half, share), BF16), vmem((chains, 3, half, share), BF16),
+        vmem((chains, 16, half, share), BF16), vmem((chains, 16, half, share), BF16),
+        vmem((chains, 2, cols, part, share), F32), vmem((chains, cols, part, share), F32),
+        vmem((chains, cols, part, share), F32), vmem((chains, cols, part, share), BF16),
+        vmem((chains, 3, part, share), BF16),
         pltpu.SemaphoreType.DMA((2 * freqs,)),
-        pltpu.SemaphoreType.DMA((76,)), pltpu.SemaphoreType.DMA((76,)),
+        pltpu.SemaphoreType.DMA((38 * chains,)), pltpu.SemaphoreType.DMA((38 * chains,)),
     ]
     in_vmem = pl.BlockSpec(memory_space=pltpu.VMEM)
     in_smem = pl.BlockSpec(memory_space=pltpu.SMEM)

time: 119 us -> 106 us (0.89)
  Pallas kernels: 114 us -> 100 us
    pallas_call x1, Pallas kernels: 114 us -> 100 us  [local(): pl.pallas_call(kernel, out_shape=(jax.ShapeDtypeStruct(model_init.shape,...]
where the time goes in v4:
time: 106 us; the launch traced here: 105 us
  Pallas kernels  100 us (94%)
  local copies, waits for them, and re-layouts  4.64 us (4%)
    pallas_call x1, Pallas kernels, local(): pl.pallas_call(kernel, out_shape=(jax.ShapeDtypeStruct(model_init.shape,...  100 us
    unnamed x10, local copies, waits for them, and re-layouts  4.64 us

profile of v4, /device:TPU:1, one launch (start us, length us, event | category | flops | bytes accessed | tf_op | source)
XLA Modules:
  0.0 105.5 jit_solution(11695413840048818573)
XLA Ops:
  0.6 0.0 copy-start
  0.6 0.9 copy-done
  1.6 0.0 copy-start.1
  1.6 0.9 copy-done.1
  2.5 0.0 copy-start.2
  2.5 0.7 copy-done.2
  3.2 0.0 copy-start.3
  3.2 0.7 copy-done.3
  3.9 100.2 %shard_map.77 = (f32[2,128,256]{2,1,0:T(8,128)S(1)}, f32[2,128,256]{2,1,0:T(8,128)S(1)}) custom-call(bf16[2,8,1024,128]{3,2,1,0:T(8,128)(2,1)} %bitcast.4, bf16[2,8,1024,128]{3,2,1,0:T(8,128)(2,1)} %bitcast.5, s32[2,4,8]{2,1,0:T(4,128)S(1)} %bitcast.3, f32[2,128,256]{2,1,0:T(8,128)S(1)} %copy-done, f32[2,128,256]{2,1,0:T(8,128)S(1)} %copy-done.1, f32[2]{0:T(128)S(1)} %copy-done.3), custom_call_target="tpu_custom_call" | custom-call | tf_op jit(solution)/shard_map/pallas_call | solution.py:396
  104.1 0.7 copy.10
  104.8 0.7 copy.11
Async XLA Ops:
  0.6 1.0 copy-start
  1.6 0.9 copy-start.1
  2.5 0.7 copy-start.2
  3.2 0.7 copy-start.3

commit v5 on v4

--- a/solution.py
+++ b/solution.py
@@ -14,17 +14,17 @@
 TRANS_B = (((1,), (1,)), ((), ()))
 SPLIT = 2
 ORDER = (
-    0, 1, 2, 3, 0, 1, 0, 1, 2, 3, 2, 3, 0, 1, 2, 3, 0,
-    1, 2, 3, 0, 1, 2, 3, 0, 1, 0, 2, 1, 3, 0, 2, 1, 3,
-    0, 2, 0, 1, 3, 1, 2, 2, 0, 3, 3, 1, 2, 0, 3, 1, 2,
-    0, 3, 1, 2, 0, 3, 0, 1, 2, 1, 0, 3, 2, 1, 3, 2, 3,
+    0, 1, 2, 3, 0, 0, 2, 2, 3, 1, 0, 3, 2, 0, 1, 2, 3,
+    0, 1, 3, 2, 0, 1, 3, 0, 2, 1, 2, 0, 3, 3, 1, 2, 0,
+    1, 0, 3, 2, 2, 1, 3, 0, 3, 1, 2, 0, 1, 3, 2, 0, 1,
+    3, 2, 1, 3, 0, 1, 2, 0, 3, 2, 1, 0, 3, 1, 2, 3, 1,
 )
 
 
 def kernel(
-    u_hbm, v_hbm, ranks, model_in, observed, step,
+    u_hbm, v_hbm, ranks, model_hbm, observed_hbm, step,
     model_out, misfit_out,
-    u_raw, v_raw, u_tiles, v_tiles, wide, expanded_f, expanded_b,
+    model_in, observed, u_raw, v_raw, u_tiles, v_tiles, wide, expanded_f, expanded_b,
     model_t, observed_t, misfit_t,
     x_all, sum_a, sum_b, got_a, got_b, keep_a, keep_b, next_a, next_b, last_a, last_b,
     r_a, r_b, grad, grad_got, grad_keep, grad_send, grad_last,
@@ -57,12 +57,18 @@
             device_id=device, device_id_type=MESH,
         )
 
+    side_loads = [
+        pltpu.make_async_copy(src, dst, load_sem.at[2 * freqs + n])
+        for n, (src, dst) in enumerate(((model_hbm, model_in), (observed_hbm, observed)))
+    ]
+    side_loads[0].start()
     loads = {}
     for f in range(freqs):
         for n, (src, dst) in enumerate(((v_hbm, v_raw), (u_hbm, u_raw))):
             loads[f, n] = pltpu.make_async_copy(src.at[f], dst.at[f], load_sem.at[2 * f + n])
             loads[f, n].start()
 
+    side_loads[1].start()
     barrier = pltpu.get_barrier_semaphore()
     peers = [at_y(o) for o in (1, 2, 3)] + [at_z(o) for o in (1, 2, 3)] + [at_x(o) for o in (1, 2, 3)] + [partner]
     for peer in peers:
@@ -79,6 +85,7 @@
         parts = [ref[SPLIT * f + h] for h in range(SPLIT)]
         return jnp.concatenate([part[:half] for part in parts] + [part[half:] for part in parts], axis=0).T
 
+    side_loads[0].wait()
     for f in range(freqs):
         for c, turned in chain_rows(f, model_in[f].T):
             model_t[c] = turned
@@ -322,18 +329,25 @@
             x_all[f, row] = new.astype(BF16)
             gather_x_start(f)
 
+    def prepare(f):
+        relayout_v(f)
+        relayout_u(f)
+        if f == 0:
+            side_loads[1].wait()
+        for c, turned in chain_rows(f, observed[f].T):
+            observed_t[c] = turned
+
     def stages(f):
         gather_x_start(f)
+        if f == chains - 1:
+            prepare(0)
         yield
         for sweep in range(ITERS):
             last = sweep == ITERS - 1
             gather_x_mid(f)
             yield
-            if sweep == 0 and f % SPLIT == 0:
-                relayout_v(f // SPLIT)
-                relayout_u(f // SPLIT)
-                for c, turned in chain_rows(f // SPLIT, observed[f // SPLIT].T):
-                    observed_t[c] = turned
+            if sweep == 0 and f % SPLIT == 0 and f > 0:
+                prepare(f // SPLIT)
             gather_x_end(f)
             forward_products(f)
             forward_sums(f)
@@ -372,7 +386,7 @@
     raw = (freqs, rows, tile * cols, width)
     vmem = lambda shape, kind: pltpu.VMEM(shape, kind)
     scratch = [
-        vmem(raw, BF16), vmem(raw, BF16),
+        vmem(model_init.shape, F32), vmem(observed.shape, F32), vmem(raw, BF16), vmem(raw, BF16),
         vmem((freqs, rows, 2 * tile, cols * width // 2), BF16), vmem((freqs, cols, 2 * tile, rows * width // 2), BF16),
         vmem((2, tile * cols, width), F32),
         vmem((rows, part, cols * width // 2), BF16), vmem((cols, part, rows * width // 2), BF16),
@@ -387,7 +401,7 @@
         vmem((chains, 2, cols, part, share), F32), vmem((chains, cols, part, share), F32),
         vmem((chains, cols, part, share), F32), vmem((chains, cols, part, share), BF16),
         vmem((chains, 3, part, share), BF16),
-        pltpu.SemaphoreType.DMA((2 * freqs,)),
+        pltpu.SemaphoreType.DMA((2 * freqs + 2,)),
         pltpu.SemaphoreType.DMA((38 * chains,)), pltpu.SemaphoreType.DMA((38 * chains,)),
     ]
     in_vmem = pl.BlockSpec(memory_space=pltpu.VMEM)
@@ -398,11 +412,11 @@
         out_shape=(
             jax.ShapeDtypeStruct(model_init.shape, F32), jax.ShapeDtypeStruct(observed.shape, F32),
         ),
-        in_specs=[anywhere, anywhere, in_smem, in_vmem, in_vmem, in_smem],
+        in_specs=[anywhere, anywhere, in_smem, anywhere, anywhere, in_smem],
         out_specs=(in_vmem, in_vmem),
         scratch_shapes=scratch,
         compiler_params=pltpu.CompilerParams(
-            collective_id=0, has_side_effects=True, vmem_limit_bytes=52 * 2**20
+            collective_id=0, has_side_effects=True, vmem_limit_bytes=int(53.25 * 2**20)
         ),
     )(u_factors.reshape(raw), v_factors.reshape(raw), ranks.transpose(0, 2, 1), model_init, observed, step)
 

time: 106 us -> 99.2 us (0.936)
  Pallas kernels: 100 us -> 95.7 us
  local copies, waits for them, and re-layouts: 4.64 us -> 2.74 us
    pallas_call x1, Pallas kernels: 100 us -> 95.7 us  [local(): pl.pallas_call(kernel, out_shape=(jax.ShapeDtypeStruct(model_init.shape,...]
    unnamed x10 -> x6, local copies, waits for them, and re-layouts: 4.64 us -> 2.74 us
where the time goes in v5:
time: 99.2 us; the launch traced here: 99.1 us
  Pallas kernels  95.7 us (96%)
  local copies, waits for them, and re-layouts  2.74 us (3%)
    pallas_call x1, Pallas kernels, local(): pl.pallas_call(kernel, out_shape=(jax.ShapeDtypeStruct(model_init.shape,...  95.7 us
    unnamed x6, local copies, waits for them, and re-layouts  2.74 us

profile of v5, /device:TPU:1, one launch (start us, length us, event | category | flops | bytes accessed | tf_op | source)
XLA Modules:
  0.0 99.1 jit_solution(11701587553990741479)
XLA Ops:
  0.6 0.0 copy-start
  0.6 0.7 copy-done
  1.3 0.0 copy-start.1
  1.3 0.7 copy-done.1
  2.0 95.7 %shard_map.77 = (f32[2,128,256]{2,1,0:T(8,128)S(1)}, f32[2,128,256]{2,1,0:T(8,128)S(1)}) custom-call(bf16[2,8,1024,128]{3,2,1,0:T(8,128)(2,1)} %bitcast.4, bf16[2,8,1024,128]{3,2,1,0:T(8,128)(2,1)} %bitcast.5, s32[2,4,8]{2,1,0:T(4,128)S(1)} %bitcast.3, f32[2,128,256]{2,1,0:T(8,128)} %model_hbm.1, f32[2,128,256]{2,1,0:T(8,128)} %observed_hbm.1, f32[2]{0:T(128)S(1)} %copy-done.1), custom_call_target="tpu_custom_call" | custom-call | tf_op jit(solution)/shard_map/pallas_call | solution.py:410
  97.7 0.7 copy.10
  98.4 0.7 copy.11
Async XLA Ops:
  0.6 0.7 copy-start
  1.3 0.7 copy-start.1

commit v6 on v5

--- a/solution.py
+++ b/solution.py
@@ -213,14 +213,14 @@
 
     def first_copies(f):
         copies = []
-        for o in (2, 1, 3):
+        for o in (1, 3, 2):
             copies.append(remote(("c1a", f, o), sum_a.at[f, pl.ds((y + o) % 4 * 4, 4)], got_a.at[f, o - 1], at_y(o)))
             copies.append(remote(("c1b", f, o), sum_b.at[f, pl.ds((z + o) % 4 * 4, 4)], got_b.at[f, o - 1], at_z(o)))
         return copies
 
     def second_copies(f):
         copies = []
-        for o in (2, 1, 3):
+        for o in (1, 3, 2):
             copies.append(remote(("c2a", f, o), next_a.at[f, (z + o) % 4], last_a.at[f, o - 1], at_z(o)))
             copies.append(remote(("c2b", f, o), next_b.at[f, (y + o) % 4], last_b.at[f, o - 1], at_y(o)))
         return copies
@@ -249,7 +249,7 @@
     def gather_first(f):
         copies = []
         own_a, own_b = r_a.at[f, y * 4 + z], r_b.at[f, z * 4 + y]
-        for o in (2, 1, 3):
+        for o in (1, 3, 2):
             copies.append(remote(("e1a", f, o), own_a, own_a, at_z(o)))
             copies.append(remote(("e1b", f, o), own_b, own_b, at_y(o)))
         return copies
@@ -257,7 +257,7 @@
     def gather_second(f):
         copies = []
         own_a, own_b = r_a.at[f, pl.ds(y * 4, 4)], r_b.at[f, pl.ds(z * 4, 4)]
-        for o in (2, 1, 3):
+        for o in (1, 3, 2):
             copies.append(remote(("e2a", f, o), own_a, own_a, at_y(o)))
             copies.append(remote(("e2b", f, o), own_b, own_b, at_z(o)))
         return copies
@@ -307,7 +307,7 @@
 
     def across_copies(f):
         return [
-            remote(("g2", f, o), grad_send.at[f, (x + o) % 4], grad_last.at[f, o - 1], at_x(o)) for o in (2, 1, 3)
+            remote(("g2", f, o), grad_send.at[f, (x + o) % 4], grad_last.at[f, o - 1], at_x(o)) for o in (1, 3, 2)
         ]
 
     def pair_end(f):

time: 99.2 us -> 98.6 us (level)
  no operation moved by 1% of the time
where the time goes in v6:
time: 98.6 us; the launch traced here: 98.4 us
  Pallas kernels  95 us (96%)
  local copies, waits for them, and re-layouts  2.74 us (3%)
    pallas_call x1, Pallas kernels, local(): pl.pallas_call(kernel, out_shape=(jax.ShapeDtypeStruct(model_init.shape,...  95 us
    unnamed x6, local copies, waits for them, and re-layouts  2.74 us

profile of v6, /device:TPU:1, one launch (start us, length us, event | category | flops | bytes accessed | tf_op | source)
XLA Modules:
  0.0 98.4 jit_solution(16016427505495886537)
XLA Ops:
  0.6 0.0 copy-start
  0.6 0.7 copy-done
  1.3 0.0 copy-start.1
  1.3 0.7 copy-done.1
  2.0 95.0 %shard_map.77 = (f32[2,128,256]{2,1,0:T(8,128)S(1)}, f32[2,128,256]{2,1,0:T(8,128)S(1)}) custom-call(bf16[2,8,1024,128]{3,2,1,0:T(8,128)(2,1)} %bitcast.4, bf16[2,8,1024,128]{3,2,1,0:T(8,128)(2,1)} %bitcast.5, s32[2,4,8]{2,1,0:T(4,128)S(1)} %bitcast.3, f32[2,128,256]{2,1,0:T(8,128)} %model_hbm.1, f32[2,128,256]{2,1,0:T(8,128)} %observed_hbm.1, f32[2]{0:T(128)S(1)} %copy-done.1), custom_call_target="tpu_custom_call" | custom-call | tf_op jit(solution)/shard_map/pallas_call | solution.py:410
  97.0 0.7 copy.10
  97.7 0.7 copy.11
Async XLA Ops:
  0.6 0.7 copy-start
  1.3 0.7 copy-start.1

commit v7 on v6

--- a/solution.py
+++ b/solution.py
@@ -234,17 +234,18 @@
             copy.wait()
 
     def first_end(f):
-        wait(first_copies(f))
-        for q in range(4):
-            for own, got, keep, onward, at in (
-                (sum_a, got_a, keep_a, next_a, y), (sum_b, got_b, keep_b, next_b, z)
-            ):
+        arriving, leaving = first_copies(f), second_copies(f)
+        for n, (own, got, keep, onward, at) in enumerate((
+            (sum_a, got_a, keep_a, next_a, y), (sum_b, got_b, keep_b, next_b, z)
+        )):
+            wait(arriving[n::2])
+            for q in range(4):
                 total = own[f, at * 4 + q].astype(F32)
                 for o in range(3):
                     total = total + got[f, o, q].astype(F32)
                 keep[f, q] = total
                 onward[f, q] = total.astype(BF16)
-        start(second_copies(f))
+            start(leaving[n::2])
 
     def gather_first(f):
         copies = []
@@ -263,11 +264,12 @@
         return copies
 
     def second_end(f, last):
-        wait(second_copies(f))
-        for keep, got, to, rows_at, at, slot in (
+        arriving, leaving = second_copies(f), gather_first(f)
+        for n, (keep, got, to, rows_at, at, slot) in enumerate((
             (keep_a, last_a, r_a, slice(0, half), z, y * 4 + z),
-            (keep_b, last_b, r_b, slice(half, tile), y, z * 4 + y),
-        ):
+            (keep_b, last_b, r_b, slice(half, 2 * half), y, z * 4 + y),
+        )):
+            wait(arriving[n::2])
             total = keep[f, at]
             for o in range(3):
                 total = total + got[f, o].astype(F32)
@@ -275,7 +277,7 @@
             if last:
                 misfit_t[f, rows_at] = total
             to[f, slot] = total.astype(BF16)
-        start(gather_first(f))
+            start(leaving[n::2])
 
     def backward_products(f):
         for p in range(rows // 2):

time: 98.6 us -> 98.6 us (level)
  no operation moved by 1% of the time
where the time goes in v7:
time: 98.6 us; the launch traced here: 98.4 us
  Pallas kernels  95 us (96%)
  local copies, waits for them, and re-layouts  2.74 us (3%)
    pallas_call x1, Pallas kernels, local(): pl.pallas_call(kernel, out_shape=(jax.ShapeDtypeStruct(model_init.shape,...  95 us
    unnamed x6, local copies, waits for them, and re-layouts  2.74 us

profile of v7, /device:TPU:1, one launch (start us, length us, event | category | flops | bytes accessed | tf_op | source)
XLA Modules:
  0.0 98.4 jit_solution(12715438246018311116)
XLA Ops:
  0.6 0.0 copy-start
  0.6 0.7 copy-done
  1.3 0.0 copy-start.1
  1.3 0.7 copy-done.1
  2.0 95.0 %shard_map.77 = (f32[2,128,256]{2,1,0:T(8,128)S(1)}, f32[2,128,256]{2,1,0:T(8,128)S(1)}) custom-call(bf16[2,8,1024,128]{3,2,1,0:T(8,128)(2,1)} %bitcast.4, bf16[2,8,1024,128]{3,2,1,0:T(8,128)(2,1)} %bitcast.5, s32[2,4,8]{2,1,0:T(4,128)S(1)} %bitcast.3, f32[2,128,256]{2,1,0:T(8,128)} %model_hbm.1, f32[2,128,256]{2,1,0:T(8,128)} %observed_hbm.1, f32[2]{0:T(128)S(1)} %copy-done.1), custom_call_target="tpu_custom_call" | custom-call | tf_op jit(solution)/shard_map/pallas_call | solution.py:412
  97.0 0.7 copy.10
  97.7 0.7 copy.11
Async XLA Ops:
  0.6 0.7 copy-start
  1.3 0.7 copy-start.1
